TPU v7x, 32 devices: a whole 2x2x4 slice. The times are simulated.
32 devices in a mesh: row: 4 (over y, core), col: 8 (over z, x).
Axes of the slice: x: 2, y: 2, z: 4, core: 2. Of those that a mesh axis runs over, the one named last changes fastest.
Arguments:
- l_saved: bfloat16 [16, 4, 256, 8, 256], P(None, 'row', None, 'col'), as said below
- l_grad: bfloat16 [16, 4, 256, 8, 256], P(None, 'row', None, 'col'), as said below
Outputs:
- grad_out: float32 [16, 4, 256, 8, 256], P(None, 'row', None, 'col')
Inputs may be any that keep to these rules, and one draw needn't show every extreme that they name: Read as one matrix of 16384 rows, l_saved is lower triangular with its diagonal between 1 and 2. Read as one matrix, l_grad is zero above the diagonal.
All inputs are finite; a program needn't handle non-finite values.
Results may differ from a plain program's by a relative error of at most 0.0003.
Values may be sent and summed in bfloat16 or wider, within the bound.
A program may use at most 64 MiB of HBM per device.

v0:
```python
import jax
import jax.numpy as jnp
from jax import lax
from jax.sharding import PartitionSpec as P

HIGH = lax.Precision.HIGHEST


def from_root(array, axis, root):
    mine = lax.axis_index(axis) == root
    return lax.psum(jnp.where(mine, array, jnp.zeros_like(array)), axis)


def right_solve(factor, rhs):
    return lax.linalg.triangular_solve(factor, rhs, left_side=False, lower=True)


def diag_gradient(factor, lower_part):
    eye = jnp.eye(factor.shape[0], dtype=jnp.float32)
    middle = jnp.dot(factor.T, lower_part, precision=HIGH, preferred_element_type=jnp.float32)
    middle = jnp.tril(middle) - 0.5 * middle * eye
    half = lax.linalg.triangular_solve(factor, middle, left_side=True, lower=True, transpose_a=True)
    full = right_solve(factor, half)
    return full + full.T


def stacked_inner(left, right):
    flat_left = left.reshape(-1, left.shape[-1])
    flat_right = right.reshape(-1, right.shape[-1]).astype(jnp.float32)
    return lax.dot_general(
        flat_left,
        flat_right,
        (((0,), (0,)), ((), ())),
        precision=HIGH,
        preferred_element_type=jnp.float32,
    )


def solve_rows(diag_factor, column, below):
    rows_here, tile = (column.shape[0], column.shape[1])
    inverse = right_solve(diag_factor, jnp.eye(tile, dtype=jnp.float32))
    solved = jnp.dot(
        column.reshape(-1, tile), inverse, precision=HIGH, preferred_element_type=jnp.float32
    ).reshape(rows_here, tile, tile)
    return jnp.where(below, solved, jnp.float32(0.0))


def diag_down(piece, owner_row):
    return from_root(piece, "row", owner_row).astype(jnp.float32)


def per_device(l_saved, l_grad):
    rows_here = l_saved.shape[0]
    tile = l_saved.shape[2]
    n_row = lax.axis_size("row")
    n_col = lax.axis_size("col")
    factor = l_saved.reshape(rows_here, tile, tile)
    grad = l_grad.reshape(rows_here, tile, tile).astype(jnp.float32)
    my_row = lax.axis_index("row")
    my_col = lax.axis_index("col")
    tile_rows = jnp.arange(rows_here, dtype=jnp.int32) * n_row + my_row
    eye = jnp.eye(tile, dtype=jnp.float32)
    for panel in (n_col - 1, n_col - 2):
        owner_row = panel % n_row
        local = panel // n_row
        at_owner = my_row == owner_row
        below = (tile_rows > panel)[:, None, None]
        diag_factor = diag_down(factor[local], owner_row)
        cbar = solve_rows(diag_factor, grad, below)
        term = jnp.where(at_owner, grad[local], jnp.float32(0.0)) - stacked_inner(cbar, factor)
        total = lax.psum(term, "row")
        sym = diag_gradient(diag_factor, jnp.tril(total))
        sent = from_root(jnp.concatenate([cbar, sym[None]], 0), "col", panel)
        cbar = sent[:rows_here]
        sym = sent[rows_here]
        row_factor = from_root(factor[local], "row", owner_row).astype(jnp.float32)
        update = jnp.dot(
            cbar.reshape(-1, tile), row_factor, precision=HIGH, preferred_element_type=jnp.float32
        )
        partial_sum = stacked_inner(cbar, factor)
        summed = lax.psum(partial_sum, "row")
        own_row = grad[local] - (
            summed + jnp.dot(sym, row_factor, precision=HIGH, preferred_element_type=jnp.float32)
        )
        updated = grad - update.reshape(rows_here, tile, tile)
        updated = updated.at[local].set(jnp.where(at_owner, own_row, updated[local]))
        abar = jnp.tril(sym) - 0.5 * sym * eye
        panel_col = jnp.where(
            below,
            cbar,
            jnp.where((tile_rows == panel)[:, None, None], abar[None], jnp.float32(0.0)),
        )
        grad = jnp.where(my_col < panel, updated, jnp.where(my_col == panel, panel_col, grad))
    return grad.reshape(l_grad.shape)


def solution(mesh):
    in_specs = (P(None, "row", None, "col", None), P(None, "row", None, "col", None))
    out_specs = P(None, "row", None, "col", None)
    return jax.shard_map(
        per_device, mesh=mesh, in_specs=in_specs, out_specs=out_specs, check_vma=False
    )
```

profile of v0, /device:TPU:0, one launch (start us, length us, event | category | flops | bytes accessed | tf_op | source)
XLA Modules:
  0.0 607.6 jit_solution(4179768059537039904)
XLA Ops:
  8.3 4.3 convert_element_type.13
  12.6 32.2 %all-reduce.21.cloned.1.call-done = (bf16[256,256]{1,0:T(8,128)(2,1)}, bf16[256,256]{1,0:T(8,128)(2,1)}) async-done(((bf16[256,256]{1,0:T(8,128)(2,1)}, bf16[256,256]{1,0:T(8,128)(2,1)}), (bf16[256,256]{1,0:T(8,128)(2,1)}, bf16[256,256]{1,0:T(8,128)(2,1)})) %all-reduce.21.cloned.1.call-update) | async-done | bytes 262160 | tf_op jit(solution)/shard_map/psum | solution.py:11
  50.1 19.7 %custom-call.10 = f32[2,128,128]{1,2,0:T(8,128)S(1)} custom-call(f32[2,128,128]{2,1,0:T(8,128)S(1)} %get-tuple-element.71), custom_call_target="InvertDiagBlocksLowerTriangular" | custom-call | tf_op jit(solution)/shard_map/triangular_solve/custom-call.1 | solution.py:15
  74.6 5.8 copy.9
  80.3 5.0 fusion.5
  85.4 4.7 broadcast_select_fusion
  90.2 27.7 %all-reduce.9.cloned.1.call-done = f32[256,256]{1,0:T(8,128)} async-done(((f32[256,256]{1,0:T(8,128)}), f32[256,256]{1,0:T(8,128)}) %all-reduce.9.cloned.1.call-update) | async-done | bytes 262160 | tf_op jit(solution)/shard_map/psum | solution.py:71
  122.8 4.7 maximum_select_fusion
  127.5 13.2 %all-reduce.13.cloned.1.call-start = ((), (), s32[]{:S(2)}) async-start(), calls=%async_computation.2 | async-start | bytes 524288 | tf_op jit(solution)/shard_map/psum | solution.py:81
  144.7 19.7 %custom-call.13 = f32[2,128,128]{1,2,0:T(8,128)S(1)} custom-call(f32[2,128,128]{2,1,0:T(8,128)S(1)} %get-tuple-element.74), custom_call_target="InvertDiagBlocksLowerTriangular" | custom-call | tf_op jit(solution)/shard_map/triangular_solve/custom-call.1 | solution.py:15
  165.3 125.3 %all-reduce.11.cloned.1.call-done = f32[17,256,256]{2,1,0:T(8,128)} async-done(((f32[17,256,256]{2,1,0:T(8,128)}), f32[17,256,256]{2,1,0:T(8,128)}) %all-reduce.11.cloned.1.call-update) | async-done | bytes 4456464 | tf_op jit(solution)/shard_map/psum | solution.py:11
  292.9 4.1 fusion.83
  297.1 4.9 bitcast_subtract_fusion
  305.0 23.4 %all-reduce.13.cloned.1.call-done = f32[256,256]{1,0:T(8,128)} async-done(((f32[256,256]{1,0:T(8,128)}), f32[256,256]{1,0:T(8,128)}) %all-reduce.13.cloned.1.call-update) | async-done | bytes 262160 | tf_op jit(solution)/shard_map/psum | solution.py:81
  330.5 5.1 fusion
  341.3 4.2 convolution_subtract_fusion.1
  345.6 31.5 %all-reduce.15.cloned.1.call-done = f32[256,256]{1,0:T(8,128)} async-done(((f32[256,256]{1,0:T(8,128)}), f32[256,256]{1,0:T(8,128)}) %all-reduce.15.cloned.1.call-update) | async-done | bytes 262160 | tf_op jit(solution)/shard_map/psum | solution.py:71
  380.3 4.7 maximum_select_fusion.1
  385.3 162.9 %all-reduce.17.cloned.1.call-done = f32[17,256,256]{2,1,0:T(8,128)} async-done(((f32[17,256,256]{2,1,0:T(8,128)}), f32[17,256,256]{2,1,0:T(8,128)}) %all-reduce.17.cloned.1.call-update) | async-done | bytes 4456464 | tf_op jit(solution)/shard_map/psum | solution.py:11
  550.4 4.1 fusion.84
  554.6 5.6 convolution_subtract_fusion
  562.3 23.7 %all-reduce.19.cloned.1.call-done = f32[256,256]{1,0:T(8,128)} async-done(((f32[256,256]{1,0:T(8,128)}), f32[256,256]{1,0:T(8,128)}) %all-reduce.19.cloned.1.call-update) | async-done | bytes 262160 | tf_op jit(solution)/shard_map/psum | solution.py:81
  588.1 5.9 select_bitcast_fusion
  594.0 6.3 %copy.7 = f32[16,1,256,1,256]{4,3,2,1,0:T(1,128)} copy(f32[16,1,256,1,256]{4,2,0,3,1:T(8,128)S(1)} %select_bitcast_fusion) | data formatting | bytes 8388608 | tf_op jit(solution)/shard_map/reshape | solution.py:94
  (98 shorter events, 52.5 us)
Async XLA Ops:
  6.5 38.3 %all-reduce.21.cloned.1.call-start = ((), (), s32[]{:S(2)}) async-start(), calls=%async_computation.6 | async-start | bytes 524288 | tf_op jit(solution)/shard_map/psum | solution.py:11
  8.2 109.7 %all-reduce.9.cloned.1.call-start = ((), (), s32[]{:S(2)}) async-start(), calls=%async_computation | async-start | bytes 524288 | tf_op jit(solution)/shard_map/psum | solution.py:71
  8.3 62.4 %copy-start.3 = (bf16[16,1,256,1,256]{4,2,3,1,0:T(8,128)(2,1)S(1)}, bf16[16,1,256,1,256]{4,2,3,1,0:T(8,128)(2,1)}, u32[]{:S(2)}) copy-start(bf16[16,1,256,1,256]{4,2,3,1,0:T(8,128)(2,1)} %param.11) | copy-start | bytes 6291460
  74.6 5.8 copy-start.2
  85.4 205.3 %all-reduce.11.cloned.1.call-start = ((), (), s32[]{:S(2)}) async-start(), calls=%async_computation.1 | async-start | bytes 8912896 | tf_op jit(solution)/shard_map/psum | solution.py:11
  85.4 32.4 %copy-start.7 = (bf16[256,256]{1,0:T(8,128)(2,1)S(1)}, bf16[256,256]{1,0:T(8,128)(2,1)}, u32[]{:S(2)}) copy-start(bf16[256,256]{1,0:T(8,128)(2,1)} %get-tuple-element.93) | copy-start | bytes 393220
  127.5 201.0 %all-reduce.13.cloned.1.call-start = ((), (), s32[]{:S(2)}) async-start(), calls=%async_computation.2 | async-start | bytes 524288 | tf_op jit(solution)/shard_map/psum | solution.py:81
  290.7 2.2 slice-start.3
  297.0 80.1 %all-reduce.15.cloned.1.call-start = ((), (), s32[]{:S(2)}) async-start(), calls=%async_computation.3 | async-start | bytes 524288 | tf_op jit(solution)/shard_map/psum | solution.py:71
  302.0 2.0 copy-start.5
  335.6 3.8 copy-start
  339.4 1.9 copy-start.1
  339.4 37.7 %copy-start.6 = (bf16[256,256]{1,0:T(8,128)(2,1)S(1)}, bf16[256,256]{1,0:T(8,128)(2,1)}, u32[]{:S(2)}) copy-start(bf16[256,256]{1,0:T(8,128)(2,1)} %get-tuple-element.94) | copy-start | bytes 393220
  345.5 202.7 %all-reduce.17.cloned.1.call-start = ((), (), s32[]{:S(2)}) async-start(), calls=%async_computation.4 | async-start | bytes 8912896 | tf_op jit(solution)/shard_map/psum | solution.py:11
  385.1 201.0 %all-reduce.19.cloned.1.call-start = ((), (), s32[]{:S(2)}) async-start(), calls=%async_computation.5 | async-start | bytes 524288 | tf_op jit(solution)/shard_map/psum | solution.py:81
  548.2 2.2 slice-start.2
  550.4 11.8 %slice-start = ((s8[4456448]{0:T(1024)(128)(4,1)}), s8[262144]{0:T(1024)(128)(4,1)S(1)}, s32[]{:S(2)}) async-start(s8[4456448]{0:T(1024)(128)(4,1)} %bitcast.165), calls=%async_computation.7 | async-start | bytes 524288
  554.6 7.7 %slice-start.1 = ((s8[4456448]{0:T(1024)(128)(4,1)}), s8[4194304]{0:T(1024)(128)(4,1)S(1)}, s32[]{:S(2)}) async-start(s8[4456448]{0:T(1024)(128)(4,1)} %bitcast.165), calls=%async_computation.8 | async-start | bytes 8388608
  560.2 2.0 copy-start.4
Sparse Core Ops, SparseCore 0:
  9.7 35.0 all-reduce.20
  85.5 32.3 all-reduce.8
  127.6 163.0 all-reduce.10
  297.1 31.2 all-reduce.12
  345.7 31.3 all-reduce.14
  385.2 163.0 all-reduce.16
  554.7 31.2 all-reduce.18
where the time goes:
time: 616 us; the launch traced here: 608 us
  waiting for transfers between devices  427 us (69%)
  other arithmetic  73.2 us (12%)
  matrix products  47.7 us (8%)
  local copies, waits for them, and re-layouts  31.8 us (5%)
  between operations  14.3 us (2%)
  starting transfers between devices  13.6 us (2%)
    psum x3, waiting for transfers between devices, from_root(): return lax.psum(jnp.where(mine, array, jnp.zeros_like(array)), axis)  320 us
    psum x2, waiting for transfers between devices, per_device(): total = lax.psum(term, 'row')  59.2 us
    psum x2, waiting for transfers between devices, per_device(): summed = lax.psum(partial_sum, 'row')  47.1 us
    another operation x6, other arithmetic, right_solve(): return lax.linalg.triangular_solve(factor, rhs, left_side=False, lower=True)  41.1 us
    dot_general x4, matrix products, stacked_inner(): lax.dot_general(flat_left, flat_right, (((0,), (0,)), ((), ())), precisio...  17.4 us
    psum x2, starting transfers between devices, per_device(): summed = lax.psum(partial_sum, 'row')  13.4 us
  transfers between devices with their start and end apart: 7, of which 7 were waited for; matrix products, arithmetic and copies ran while one was open for 7% of the time, Pallas kernels for 0%

commit v1 on v0

--- a/solution.py
+++ b/solution.py
@@ -68,7 +68,7 @@
         diag_factor = diag_down(factor[local], owner_row)
         cbar = solve_rows(diag_factor, grad, below)
         term = jnp.where(at_owner, grad[local], jnp.float32(0.0)) - stacked_inner(cbar, factor)
-        total = lax.psum(term, "row")
+        total = jnp.sum(lax.all_gather(term, "row"), axis=0)
         sym = diag_gradient(diag_factor, jnp.tril(total))
         sent = from_root(jnp.concatenate([cbar, sym[None]], 0), "col", panel)
         cbar = sent[:rows_here]

time: 616 us -> 580 us (0.942)
  waiting for transfers between devices: 427 us -> 390 us
    psum x2 -> x0, waiting for transfers between devices: 59.2 us -> none  [per_device(): total = lax.psum(term, 'row')]
    all_gather x0 -> x2, waiting for transfers between devices: none -> 22.1 us  [per_device(): total = jnp.sum(lax.all_gather(term, 'row'), axis=0)]
  transfers between devices with their start and end apart: 7 -> 7, of which waited for: 7 -> 7; matrix products, arithmetic and copies ran while one was open for 7% -> 9% of each run, Pallas kernels for 0% -> 0%
where the time goes in v1:
time: 580 us; the launch traced here: 572 us
  waiting for transfers between devices  390 us (67%)
  other arithmetic  75.8 us (13%)
  matrix products  44.3 us (8%)
  local copies, waits for them, and re-layouts  33.8 us (6%)
  between operations  14.3 us (2%)
  starting transfers between devices  13.6 us (2%)
    psum x3, waiting for transfers between devices, from_root(): return lax.psum(jnp.where(mine, array, jnp.zeros_like(array)), axis)  320 us
    psum x2, waiting for transfers between devices, per_device(): summed = lax.psum(partial_sum, 'row')  47.1 us
    another operation x6, other arithmetic, right_solve(): return lax.linalg.triangular_solve(factor, rhs, left_side=False, lower=True)  41.1 us
    all_gather x2, waiting for transfers between devices, per_device(): total = jnp.sum(lax.all_gather(term, 'row'), axis=0)  22.1 us
    dot_general x4, matrix products, stacked_inner(): lax.dot_general(flat_left, flat_right, (((0,), (0,)), ((), ())), precisio...  16.3 us
    psum x2, starting transfers between devices, per_device(): summed = lax.psum(partial_sum, 'row')  13.5 us
  transfers between devices with their start and end apart: 7, of which 7 were waited for; matrix products, arithmetic and copies ran while one was open for 9% of the time, Pallas kernels for 0%

profile of v1, /device:TPU:0, one launch (start us, length us, event | category | flops | bytes accessed | tf_op | source)
XLA Modules:
  0.0 571.8 jit_solution(4807855089653112688)
XLA Ops:
  12.4 32.4 %all-reduce.15.cloned.1.call-done = (bf16[256,256]{1,0:T(8,128)(2,1)}, bf16[256,256]{1,0:T(8,128)(2,1)}) async-done(((bf16[256,256]{1,0:T(8,128)(2,1)}, bf16[256,256]{1,0:T(8,128)(2,1)}), (bf16[256,256]{1,0:T(8,128)(2,1)}, bf16[256,256]{1,0:T(8,128)(2,1)})) %all-reduce.15.cloned.1.call-update) | async-done | bytes 262160 | tf_op jit(solution)/shard_map/psum | solution.py:11
  45.9 4.1 while.14
  50.1 19.7 %custom-call.10 = f32[2,128,128]{1,2,0:T(8,128)S(1)} custom-call(f32[2,128,128]{2,1,0:T(8,128)S(1)} %get-tuple-element.71), custom_call_target="InvertDiagBlocksLowerTriangular" | custom-call | tf_op jit(solution)/shard_map/triangular_solve/custom-call.1 | solution.py:15
  80.2 5.7 copy.9
  85.9 4.9 broadcast_select_fusion
  90.8 6.2 %all-gather.5.cloned.1.call-done = f32[1024,256]{1,0:T(8,128)} async-done(((f32[256,256]{1,0:T(8,128)}), f32[1024,256]{1,0:T(8,128)}) %all-gather.5.cloned.1.call-update) | async-done | bytes 1048592 | tf_op jit(solution)/shard_map/all_gather | solution.py:71
  102.3 4.7 maximum_select_fusion
  107.0 13.2 %all-reduce.9.cloned.1.call-start = ((), (), s32[]{:S(2)}) async-start(), calls=%async_computation.1 | async-start | bytes 524288 | tf_op jit(solution)/shard_map/psum | solution.py:81
  120.3 4.1 while.15
  124.4 19.7 %custom-call.13 = f32[2,128,128]{1,2,0:T(8,128)S(1)} custom-call(f32[2,128,128]{2,1,0:T(8,128)S(1)} %get-tuple-element.74), custom_call_target="InvertDiagBlocksLowerTriangular" | custom-call | tf_op jit(solution)/shard_map/triangular_solve/custom-call.1 | solution.py:15
  145.0 125.1 %all-reduce.7.cloned.1.call-done = f32[17,256,256]{2,1,0:T(8,128)} async-done(((f32[17,256,256]{2,1,0:T(8,128)}), f32[17,256,256]{2,1,0:T(8,128)}) %all-reduce.7.cloned.1.call-update) | async-done | bytes 4456464 | tf_op jit(solution)/shard_map/psum | solution.py:11
  272.3 4.1 fusion.83
  276.5 4.9 bitcast_subtract_fusion
  284.5 23.4 %all-reduce.9.cloned.1.call-done = f32[256,256]{1,0:T(8,128)} async-done(((f32[256,256]{1,0:T(8,128)}), f32[256,256]{1,0:T(8,128)}) %all-reduce.9.cloned.1.call-update) | async-done | bytes 262160 | tf_op jit(solution)/shard_map/psum | solution.py:81
  310.0 5.1 fusion
  320.8 4.2 convolution_subtract_fusion.1
  325.1 15.9 %all-gather.7.cloned.1.call-done = f32[1024,256]{1,0:T(8,128)} async-done(((f32[256,256]{1,0:T(8,128)}), f32[1024,256]{1,0:T(8,128)}) %all-gather.7.cloned.1.call-update) | async-done | bytes 1048592 | tf_op jit(solution)/shard_map/all_gather | solution.py:71
  344.6 4.7 maximum_select_fusion.1
  349.6 162.9 %all-reduce.11.cloned.1.call-done = f32[17,256,256]{2,1,0:T(8,128)} async-done(((f32[17,256,256]{2,1,0:T(8,128)}), f32[17,256,256]{2,1,0:T(8,128)}) %all-reduce.11.cloned.1.call-update) | async-done | bytes 4456464 | tf_op jit(solution)/shard_map/psum | solution.py:11
  514.7 4.1 fusion.84
  518.9 5.6 convolution_subtract_fusion
  526.6 23.7 %all-reduce.13.cloned.1.call-done = f32[256,256]{1,0:T(8,128)} async-done(((f32[256,256]{1,0:T(8,128)}), f32[256,256]{1,0:T(8,128)}) %all-reduce.13.cloned.1.call-update) | async-done | bytes 262160 | tf_op jit(solution)/shard_map/psum | solution.py:81
  552.4 5.9 %select_bitcast_fusion = f32[16,1,256,1,256]{4,2,0,3,1:T(8,128)S(1)} fusion(f32[16,256,256]{2,1,0:T(8,128)} %fusion.15, f32[16,256,256]{2,1,0:T(8,128)} %copy-done, f32[256,256]{1,0:T(8,128)S(1)} %subtract_bitcast_fusion, pred[16]{0:T(512)(128)(4,1)S(1)} %broadcast_compare_fusion, pred[16]{0:T(512)(128)(4,1)S(1)} %get-tuple-element.101, pred[]{:T(512)S(6)} %eq.62, ...), kind=kLoop, calls=%fused_computation.10 | loop fusion | flops 4194304 | bytes 17039394 | tf_op jit(solution)/shard_map/reshape | solution.py:94
  558.3 6.3 %copy.7 = f32[16,1,256,1,256]{4,3,2,1,0:T(1,128)} copy(f32[16,1,256,1,256]{4,2,0,3,1:T(8,128)S(1)} %select_bitcast_fusion) | data formatting | bytes 8388608 | tf_op jit(solution)/shard_map/reshape | solution.py:94
  (100 shorter events, 54.9 us)
Async XLA Ops:
  6.5 38.3 %all-reduce.15.cloned.1.call-start = ((), (), s32[]{:S(2)}) async-start(), calls=%async_computation.6 | async-start | bytes 524288 | tf_op jit(solution)/shard_map/psum | solution.py:11
  8.2 88.8 %all-gather.5.cloned.1.call-start = ((), (), s32[]{:S(2)}) async-start(), calls=%async_computation.4 | async-start | bytes 1310720 | tf_op jit(solution)/shard_map/all_gather | solution.py:71
  45.9 30.3 %copy-start.3 = (bf16[16,1,256,1,256]{4,2,3,1,0:T(8,128)(2,1)S(1)}, bf16[16,1,256,1,256]{4,2,3,1,0:T(8,128)(2,1)}, u32[]{:S(2)}) copy-start(bf16[16,1,256,1,256]{4,2,3,1,0:T(8,128)(2,1)} %param.10) | copy-start | bytes 6291460
  74.3 1.9 copy-start.2
  80.1 190.0 %all-reduce.7.cloned.1.call-start = ((), (), s32[]{:S(2)}) async-start(), calls=%async_computation | async-start | bytes 8912896 | tf_op jit(solution)/shard_map/psum | solution.py:11
  85.9 12.4 %copy-start.7 = (bf16[256,256]{1,0:T(8,128)(2,1)S(1)}, bf16[256,256]{1,0:T(8,128)(2,1)}, u32[]{:S(2)}) copy-start(bf16[256,256]{1,0:T(8,128)(2,1)} %get-tuple-element.93) | copy-start | bytes 393220
  107.0 200.9 %all-reduce.9.cloned.1.call-start = ((), (), s32[]{:S(2)}) async-start(), calls=%async_computation.1 | async-start | bytes 524288 | tf_op jit(solution)/shard_map/psum | solution.py:81
  270.2 2.2 slice-start.3
  276.5 64.5 %all-gather.7.cloned.1.call-start = ((), (), s32[]{:S(2)}) async-start(), calls=%async_computation.5 | async-start | bytes 1310720 | tf_op jit(solution)/shard_map/all_gather | solution.py:71
  281.5 2.0 copy-start.5
  315.1 3.8 copy-start
  318.9 1.9 copy-start.1
  320.8 21.5 %copy-start.6 = (bf16[256,256]{1,0:T(8,128)(2,1)S(1)}, bf16[256,256]{1,0:T(8,128)(2,1)}, u32[]{:S(2)}) copy-start(bf16[256,256]{1,0:T(8,128)(2,1)} %get-tuple-element.94) | copy-start | bytes 393220
  325.0 187.5 %all-reduce.11.cloned.1.call-start = ((), (), s32[]{:S(2)}) async-start(), calls=%async_computation.2 | async-start | bytes 8912896 | tf_op jit(solution)/shard_map/psum | solution.py:11
  349.3 201.0 %all-reduce.13.cloned.1.call-start = ((), (), s32[]{:S(2)}) async-start(), calls=%async_computation.3 | async-start | bytes 524288 | tf_op jit(solution)/shard_map/psum | solution.py:81
  512.5 2.2 slice-start.2
  514.7 11.8 %slice-start = ((s8[4456448]{0:T(1024)(128)(4,1)}), s8[262144]{0:T(1024)(128)(4,1)S(1)}, s32[]{:S(2)}) async-start(s8[4456448]{0:T(1024)(128)(4,1)} %bitcast.167), calls=%async_computation.7 | async-start | bytes 524288
  518.8 7.7 %slice-start.1 = ((s8[4456448]{0:T(1024)(128)(4,1)}), s8[4194304]{0:T(1024)(128)(4,1)S(1)}, s32[]{:S(2)}) async-start(s8[4456448]{0:T(1024)(128)(4,1)} %bitcast.167), calls=%async_computation.8 | async-start | bytes 8388608
  524.5 2.0 copy-start.4
Sparse Core Ops, SparseCore 0:
  9.7 35.0 all-reduce.14
  80.2 16.6 all-gather.4
  107.1 162.9 all-reduce.6
  276.6 31.2 all-reduce.8
  325.1 15.7 all-gather.6
  349.5 163.0 all-reduce.10
  519.0 31.2 all-reduce.12
